TPU v7x, 512 devices: a whole 4x8x8 slice. The times are simulated.
512 devices in a mesh: rows: 64 (over z, y), cent: 8 (over x, core).
Axes of the slice: x: 4, y: 8, z: 8, core: 2. Of those that a mesh axis runs over, the one named last changes fastest.
Arguments:
- points: bfloat16 [65536, 1024], P('rows'), may hold values from -8 to 8
- centroids: bfloat16 [4096, 1024], P('cent'), may hold values from -8 to 8
- assign: int32 [65536], P('rows'), may hold values from 0 to 4095, as said below
Outputs:
- nearest: float32 [2, 65536], P(None, 'rows')
- updated: bfloat16 [4096, 1024], P('cent')
Inputs may be any that keep to these rules, and one draw needn't show every extreme that they name: `assign`: split the points into aligned blocks of 1024 and the centroids into aligned groups of 8 consecutive ones: in each block at most 4 points are assigned into any one group, and in every block some group takes exactly 4 of them.
All inputs are finite; a program needn't handle non-finite values.
Results may differ from a plain program's by a relative error of at most 0.001.
Values may be sent and summed in bfloat16 or wider, within the bound.
A program may use at most 64 MiB of HBM per device.

v0:
```python
import jax
import jax.numpy as jnp
from jax import lax
from jax.sharding import PartitionSpec as P


def in_one_piece(arrays, axis, split_dim, concat_dim, along):
    columns = [a.reshape(*a.shape[:along], -1) for a in arrays]
    both = jnp.concatenate(columns, axis=along)
    out, at, outs = (
        lax.all_to_all(both, axis, split_axis=split_dim, concat_axis=concat_dim, tiled=True),
        0,
        [],
    )
    for a, column in zip(arrays, columns):
        piece = out[..., at : at + column.shape[along]]
        outs.append(piece.reshape(*piece.shape[:along], *a.shape[along:]))
        at += column.shape[along]
    return tuple(outs)


def in_order(tiles, dim):
    dims = list(tiles.shape[1:])
    dims[dim] *= tiles.shape[0]
    return jnp.moveaxis(tiles, 0, dim).reshape(dims)


def copy_for_each(shard, axis):
    length = lax.axis_size(axis)
    return lax.all_to_all(
        jnp.broadcast_to(shard[None], (length, *shard.shape)), axis, 0, 0, tiled=True
    )


def gathered_copies(shard, axis, dim):
    return in_order(copy_for_each(shard, axis), dim)


def of_everyone(shard, axis):
    return copy_for_each(shard, axis).min(axis=0)


def smallest(points, pnorm, cents):
    cnorm = jnp.sum(jnp.square(cents.astype(jnp.float32)), axis=1)
    dots = lax.dot_general(
        points, cents, (((1,), (1,)), ((), ())), preferred_element_type=jnp.float32
    )
    return jnp.min((pnorm[:, None] - 2.0 * dots + cnorm[None, :]) / points.shape[1], axis=1)


def renew(part_sums, part_counts, own_rows):
    return ((part_sums + own_rows.astype(jnp.float32)) / (part_counts[:, None] + 1.0)).astype(
        jnp.bfloat16
    )


def per_device(points, centroids, assign):
    blocksize = centroids.shape[0]
    count_pts = points.shape[0]
    pnorm = jnp.sum(jnp.square(points.astype(jnp.float32)), axis=1)
    first = smallest(points, pnorm, centroids)
    relative = assign - lax.axis_index("cent") * blocksize
    share = blocksize // lax.axis_size("rows")
    own = lax.dynamic_slice_in_dim(centroids, lax.axis_index("rows") * share, share, 0)
    rows_count = lax.axis_size("rows")
    groups = rows_count * lax.axis_size("cent")
    capacity = max(2, 2 * count_pts // groups)
    inside = (relative >= 0) & (relative < blocksize)
    owners = jnp.where(inside, relative // share, rows_count)
    offsets = jnp.where(inside, relative - relative // share * share, 0)
    owner_hot = owners[:, None] == lax.broadcasted_iota(jnp.int32, (count_pts, rows_count), 1)
    earlier = lax.broadcasted_iota(jnp.int32, (count_pts, count_pts), 1) < lax.broadcasted_iota(
        jnp.int32, (count_pts, count_pts), 0
    )
    before = jnp.dot(
        earlier.astype(jnp.bfloat16),
        owner_hot.astype(jnp.bfloat16),
        preferred_element_type=jnp.float32,
    )
    ranking = jnp.sum(jnp.where(owner_hot, before, 0.0), axis=1).astype(jnp.int32)
    slot_index = jnp.where(inside, owners * capacity + ranking, -1)
    placing = (
        lax.broadcasted_iota(jnp.int32, (rows_count * capacity, count_pts), 0)
        == slot_index[None, :]
    )
    outgoing = jnp.dot(
        placing.astype(jnp.bfloat16), points, preferred_element_type=jnp.float32
    ).astype(jnp.bfloat16)
    labels = (jnp.sum(jnp.where(placing, offsets[None, :] + 1, 0), axis=1) - 1).astype(jnp.bfloat16)
    arrived, arrived_labels = in_one_piece((outgoing, labels), "rows", 0, 0, 1)
    chosen = (
        lax.broadcasted_iota(jnp.int32, (share, arrived.shape[0]), 0)
        == arrived_labels.astype(jnp.int32)[None, :]
    )
    part_sums = jnp.dot(chosen.astype(jnp.bfloat16), arrived, preferred_element_type=jnp.float32)
    part_counts = jnp.sum(chosen.astype(jnp.float32), axis=1)
    updated = gathered_copies(renew(part_sums, part_counts, own), "rows", 0)
    second = smallest(points, pnorm, updated)
    nearest = of_everyone(jnp.stack([first, second]), "cent")
    return (nearest, updated)


def solution(mesh):
    return jax.shard_map(
        per_device,
        mesh=mesh,
        in_specs=(P("rows", None), P("cent", None), P("rows")),
        out_specs=(P(None, "rows"), P("cent", None)),
        check_vma=False,
    )
```

profile of v0, /device:TPU:1, one launch (start us, length us, event | category | flops | bytes accessed | tf_op | source)
XLA Modules:
  0.0 94.9 jit_solution(3433765665574337176)
XLA Ops:
  0.6 0.7 broadcast_select_fusion
  1.3 0.6 fusion.2
  1.9 0.7 add_select_fusion.1
  2.6 0.2 select_reduce_fusion
  2.8 0.2 convert_element_type.66
  3.1 2.3 %convolution_convert_fusion = bf16[256,1024]{1,0:T(8,128)(2,1)S(1)} fusion(bf16[1024,1024]{1,0:T(8,128)(2,1)} %param.3, s32[1024]{0:T(1024)S(1)} %get-tuple-element.2), kind=kOutput, calls=%fused_computation.7 | convolution fusion | flops 537395200 | bytes 2625536 | tf_op jit(solution)/shard_map/dot_general | solution.py:86
  5.4 0.2 concatenate.6
  5.6 1.1 %pad_maximum_fusion = bf16[64,4,1025]{2,1,0:T(4,128)(2,1)} fusion(bf16[64,4,1]{2,1,0:T(4,128)(2,1)S(1)} %convert_element_type.66, bf16[64,4,1024]{2,1,0:T(4,128)(2,1)S(1)} %concatenate.6), kind=kLoop, calls=%fused_computation.15 | loop fusion | flops 1049600 | bytes 1049600 | tf_op jit(solution)/shard_map/concatenate | solution.py:9
  6.7 17.1 %all-to-all-start = ((bf16[64,4,1025]{2,1,0:T(4,128)(2,1)}), bf16[64,4,1025]{2,1,0:T(4,128)(2,1)S(1)}, u32[]{:S(2)}, u32[]{:S(2)}) async-start(bf16[64,4,1025]{2,1,0:T(4,128)(2,1)} %pad_maximum_fusion), calls=%async_computation | async-start | bytes 1179648 | tf_op jit(solution)/shard_map/all_to_all | solution.py:11
  23.8 17.9 %all-to-all-done = bf16[64,4,1025]{2,1,0:T(4,128)(2,1)S(1)} async-done(((bf16[64,4,1025]{2,1,0:T(4,128)(2,1)}), bf16[64,4,1025]{2,1,0:T(4,128)(2,1)S(1)}, u32[]{:S(2)}, u32[]{:S(2)}) %all-to-all-start) | async-done | bytes 524832 | tf_op jit(solution)/shard_map/all_to_all | solution.py:11
  41.8 0.3 all_to_all.13
  42.2 0.1 convert_reduce_fusion.1
  42.3 0.9 fusion.4
  43.2 1.1 %broadcast_in_dim.47 = bf16[64,8,1024]{2,1,0:T(8,128)(2,1)} broadcast(bf16[8,1024]{1,0:T(8,128)(2,1)S(1)} %fusion.4), dimensions={1,2} | broadcast | bytes 1064960 | tf_op jit(solution)/shard_map/broadcast_in_dim | solution.py:31
  44.3 7.5 %all-to-all-start.1 = ((bf16[64,8,1024]{2,1,0:T(8,128)(2,1)}), bf16[64,8,1024]{2,1,0:T(8,128)(2,1)S(1)}, u32[]{:S(2)}, u32[]{:S(2)}) async-start(bf16[64,8,1024]{2,1,0:T(8,128)(2,1)} %broadcast_in_dim.47), calls=%async_computation.1 | async-start | bytes 2097152 | tf_op jit(solution)/shard_map/all_to_all | solution.py:30
  51.8 1.6 %multiply_reduce_fusion.4 = f32[512]{0:T(512)S(1)} fusion(bf16[512,1024]{1,0:T(8,128)(2,1)} %param.4), kind=kLoop, calls=%fused_computation.6 | loop fusion | flops 1572352 | bytes 1050624 | tf_op jit(solution)/shard_map/reduce_sum | solution.py:44
  53.4 0.5 multiply_reduce_fusion
  53.9 1.4 %multiply_reduce_fusion.3 = f32[1024]{0:T(1024)S(1)} fusion(bf16[1024,1024]{1,0:T(8,128)(2,1)S(1)} %copy-done, bf16[512,1024]{1,0:T(8,128)(2,1)S(1)} %copy-done.1, f32[512]{0:T(512)S(1)} %multiply_reduce_fusion.4, f32[1024]{0:T(1024)S(1)} %multiply_reduce_fusion), kind=kOutput, calls=%fused_computation.5 | convolution fusion | flops 1076362240 | bytes 3155968 | tf_op jit(solution)/shard_map/dot_general | solution.py:45
  55.3 23.0 %all-to-all-done.1 = bf16[64,8,1024]{2,1,0:T(8,128)(2,1)S(1)} async-done(((bf16[64,8,1024]{2,1,0:T(8,128)(2,1)}), bf16[64,8,1024]{2,1,0:T(8,128)(2,1)S(1)}, u32[]{:S(2)}, u32[]{:S(2)}) %all-to-all-start.1) | async-done | bytes 1048608 | tf_op jit(solution)/shard_map/all_to_all | solution.py:30
  78.4 0.3 multiply_reduce_fusion.2
  78.7 1.4 %multiply_reduce_fusion.1 = f32[1024]{0:T(1024)S(1)} fusion(bf16[512,1024]{1,0:T(8,128)(2,1)S(1)} %bitcast.8, bf16[1024,1024]{1,0:T(8,128)(2,1)S(1)} %copy-done, f32[512]{0:T(512)S(1)} %add.59, f32[1024]{0:T(1024)S(1)} %multiply_reduce_fusion), kind=kOutput, calls=%fused_computation.3 | convolution fusion | flops 1076362240 | bytes 3155968 | tf_op jit(solution)/shard_map/dot_general | solution.py:45
  80.2 13.2 %all_to_all.19 = f32[8,2,1024]{2,1,0:T(2,128)S(1)} all-to-all(f32[8,2,1024]{2,1,0:T(2,128)S(1)} %broadcast_in_dim.48), channel_id=1, replica_groups=mesh['rows'=64,'cent'=8] {'cent'}, dimensions={0} | all-to-all | bytes 131072 | tf_op jit(solution)/shard_map/all_to_all | solution.py:30
  93.3 0.6 reduce_min.29
  94.0 1.0 %copy.11 = bf16[512,1024]{1,0:T(8,128)(2,1)} copy(bf16[512,1024]{1,0:T(8,128)(2,1)S(1)} %bitcast.9) | data formatting | bytes 2097152
  (10 shorter events, 0.3 us)
Async XLA Ops:
  6.7 35.1 %all-to-all-start = ((bf16[64,4,1025]{2,1,0:T(4,128)(2,1)}), bf16[64,4,1025]{2,1,0:T(4,128)(2,1)S(1)}, u32[]{:S(2)}, u32[]{:S(2)}) async-start(bf16[64,4,1025]{2,1,0:T(4,128)(2,1)} %pad_maximum_fusion), calls=%async_computation | async-start | bytes 1179648 | tf_op jit(solution)/shard_map/all_to_all | solution.py:11
  43.2 10.2 %copy-start = (bf16[1024,1024]{1,0:T(8,128)(2,1)S(1)}, bf16[1024,1024]{1,0:T(8,128)(2,1)}, u32[]{:S(2)}) copy-start(bf16[1024,1024]{1,0:T(8,128)(2,1)} %param.3) | copy-start | bytes 6291460
  44.3 34.0 %all-to-all-start.1 = ((bf16[64,8,1024]{2,1,0:T(8,128)(2,1)}), bf16[64,8,1024]{2,1,0:T(8,128)(2,1)S(1)}, u32[]{:S(2)}, u32[]{:S(2)}) async-start(bf16[64,8,1024]{2,1,0:T(8,128)(2,1)} %broadcast_in_dim.47), calls=%async_computation.1 | async-start | bytes 2097152 | tf_op jit(solution)/shard_map/all_to_all | solution.py:30
  51.8 2.1 %copy-start.1 = (bf16[512,1024]{1,0:T(8,128)(2,1)S(1)}, bf16[512,1024]{1,0:T(8,128)(2,1)}, u32[]{:S(2)}) copy-start(bf16[512,1024]{1,0:T(8,128)(2,1)} %param.4) | copy-start | bytes 3145732
where the time goes:
time: 95.5 us; the launch traced here: 94.9 us
  waiting for transfers between devices  41 us (43%)
  starting transfers between devices  24.6 us (26%)
  blocking collectives  13.2 us (14%)
  matrix products  6.57 us (7%)
  other arithmetic  5.92 us (6%)
  local copies, waits for them, and re-layouts  2.92 us (3%)
    all_to_all x1, waiting for transfers between devices, copy_for_each(): lax.all_to_all(jnp.broadcast_to(shard[None], (length, *shard.shape)), axi...  23 us
    all_to_all x1, waiting for transfers between devices, in_one_piece(): lax.all_to_all(both, axis, split_axis=split_dim, concat_axis=concat_dim,...  17.9 us
    all_to_all x1, starting transfers between devices, in_one_piece(): lax.all_to_all(both, axis, split_axis=split_dim, concat_axis=concat_dim,...  17.1 us
    all_to_all x1, blocking collectives, copy_for_each(): lax.all_to_all(jnp.broadcast_to(shard[None], (length, *shard.shape)), axi...  13.2 us
    all_to_all x1, starting transfers between devices, copy_for_each(): lax.all_to_all(jnp.broadcast_to(shard[None], (length, *shard.shape)), axi...  7.49 us
    dot_general x2, matrix products, smallest(): lax.dot_general(points, cents, (((1,), (1,)), ((), ())), preferred_elemen...  2.78 us
    dot_general x1, matrix products, per_device(): jnp.dot(placing.astype(jnp.bfloat16), points, preferred_element_type=jnp....  2.31 us
  transfers between devices with their start and end apart: 2, of which 2 were waited for; matrix products, arithmetic and copies ran while one was open for 4% of the time, Pallas kernels for 0%

commit v1 on v0

v1 whole, which is shorter than its diff:
```python
import functools

import jax
import jax.numpy as jnp
from jax import lax
from jax.experimental import pallas as pl
from jax.experimental.pallas import tpu as pltpu
from jax.sharding import PartitionSpec as P

MESH = pl.DeviceIdType.MESH
F32 = jnp.float32
BF16 = jnp.bfloat16
RING = 8
HALF = RING // 2
SHARE = 8
CAP = 4
LANES = 128
NT = (((1,), (1,)), ((), ()))
ORDER = (4, 3, 5, 2, 6, 1, 7)


def iota(shape, dim):
    return lax.broadcasted_iota(jnp.int32, shape, dim)


def kernel(
    points_hbm, cents_hbm, assign_ref, nearest_ref, updated_hbm,
    pts, cents, place, slots, labels, got, got_labels, part, parts, new, best, bests, pnorm,
    local_sem, out_sem, s1_send, s1_recv, l1_send, l1_recv, s2_send, s2_recv,
    g1_send, g1_recv, g2_send, g2_recv, c_send, c_recv,
):
    n_pts, width = points_hbm.shape
    blocks = n_pts // LANES
    row = lax.axis_index("rows")
    cent = lax.axis_index("cent")
    z = row // RING
    y = row % RING
    par = (z + y) % 2
    pos = (y, z)
    n_cent = bests.shape[1]

    def at(route, p):
        return z * RING + p if route == 0 else p * RING + y

    load_pts = pltpu.make_async_copy(points_hbm, pts, local_sem.at[0])
    load_cents = pltpu.make_async_copy(cents_hbm, cents, local_sem.at[1])
    load_pts.start()
    load_cents.start()

    barrier = pltpu.get_barrier_semaphore()
    for route in (0, 1):
        for i in ORDER:
            pl.semaphore_signal(
                barrier, inc=1, device_id={"rows": at(route, (pos[route] + i) % RING)}, device_id_type=MESH
            )
    for i in range(1, n_cent):
        pl.semaphore_signal(barrier, inc=1, device_id={"cent": (cent + i) % n_cent}, device_id_type=MESH)

    rel = assign_ref[...] - cent * (RING * RING * SHARE)
    inside = (rel >= 0) & (rel < RING * RING * SHARE)
    owner = jnp.where(inside, rel // SHARE, -1)
    label = jnp.where(inside, rel % SHARE + 1, 0).astype(F32)
    oz = owner // RING
    oy = owner % RING
    kind = (oz + oy) % 2
    prim = jnp.where(kind == 0, oy, oz)
    sec = jnp.where(kind == 0, oz, oy) // 2
    me_lane = jnp.where(kind == 0, y, z) * (HALF * CAP)

    groups = iota((RING * RING, LANES), 0)
    hots = [(groups == owner[b : b + 1, :]).astype(F32) for b in range(blocks)]
    upper = (iota((LANES, LANES), 0) < iota((LANES, LANES), 1)).astype(BF16)
    within = jnp.dot(
        jnp.concatenate(hots, axis=0).astype(BF16), upper, preferred_element_type=F32
    )
    carry = jnp.zeros((RING * RING, 1), F32)
    marks, spots = [], []
    for b in range(blocks):
        before = within[b * RING * RING : (b + 1) * RING * RING] + carry
        rank = jnp.sum(hots[b] * before, axis=0, keepdims=True).astype(jnp.int32)
        carry = carry + jnp.sum(hots[b], axis=1, keepdims=True)
        ins, knd, prm = inside[b : b + 1, :], kind[b : b + 1, :], prim[b : b + 1, :]
        spot = sec[b : b + 1, :] * CAP + rank
        slot = jnp.where(ins, (knd * RING + prm) * (HALF * CAP) + spot, -1)
        columns = slice(b * LANES, (b + 1) * LANES)
        place[:, columns] = (iota((place.shape[0], LANES), 0) == slot).astype(F32).astype(BF16)
        marks.append(
            jnp.where(
                iota((2 * RING, LANES), 0) == jnp.where(ins, knd * RING + prm, -1), label[b : b + 1, :], 0.0
            )
        )
        spots.append((iota((LANES, LANES), 0) == me_lane[b : b + 1, :] + spot).astype(F32))
    mine = lax.dot_general(
        jnp.concatenate(marks, axis=1).astype(BF16),
        jnp.concatenate(spots, axis=1).astype(BF16),
        NT,
        preferred_element_type=F32,
    )
    for d in range(2 * RING):
        labels[d] = mine[d : d + 1, :]

    load_pts.wait()
    tile = 256

    def place_tile(i, _):
        columns = pl.ds(pl.multiple_of(i * tile, tile), tile)
        rows = jnp.dot(place[...], pts[:, columns], preferred_element_type=F32).astype(BF16)
        slots[:, :, columns] = rows.reshape(2 * RING, HALF * CAP, tile)
        return 0

    lax.fori_loop(0, width // tile, place_tile, 0)

    pl.semaphore_wait(barrier, 2 * (RING - 1) + n_cent - 1)

    def stage1(route, i):
        to = (pos[route] + i) % RING
        who = {"rows": at(route, to)}
        return (
            pltpu.make_async_remote_copy(
                labels.at[route * RING + to], got_labels.at[route, pos[route]],
                l1_send.at[route, i], l1_recv.at[route, i], who, MESH,
            ),
            pltpu.make_async_remote_copy(
                slots.at[route * RING + to], got.at[route, pos[route]],
                s1_send.at[route, i], s1_recv.at[route, i], who, MESH,
            ),
        )

    for i in ORDER:
        for route in (0, 1):
            for copy in stage1(route, i):
                copy.start()
    for route in (0, 1):
        got_labels[route, pos[route]] = labels[route * RING + pos[route]]
        got[route, pos[route]] = slots[route * RING + pos[route]]

    load_cents.wait()
    chunk = 8

    def smallest(block, low):
        dots = lax.dot_general(block, pts[...], NT, preferred_element_type=F32)
        wide = block.astype(F32)
        norm = jnp.sum(wide * wide, axis=1, keepdims=True)
        return jnp.minimum(low, jnp.min(norm - 2.0 * dots, axis=0, keepdims=True))

    def first_tile(i, low):
        block = cents[pl.ds(i * chunk, chunk)].reshape(chunk * SHARE, width)
        return smallest(block, low)

    none = jnp.full((1, n_pts), jnp.inf, F32)
    best[0] = lax.fori_loop(0, RING * RING // chunk, first_tile, none)
    bests[0, cent] = best[0]

    def norm_tile(i, _):
        rows = pl.ds(pl.multiple_of(i * LANES, LANES), LANES)
        wide = pts[rows, :].astype(F32)
        total = jnp.sum(wide * wide, axis=1, keepdims=True)
        pnorm[:, rows] = jnp.transpose(jnp.broadcast_to(total, (LANES, LANES)))[0:1, :]
        return 0

    lax.fori_loop(0, blocks, norm_tile, 0)

    def across(which, i):
        return pltpu.make_async_remote_copy(
            best.at[which], bests.at[which, cent], c_send.at[which, i], c_recv.at[which, i],
            {"cent": (cent + i) % n_cent}, MESH,
        )

    for route in (0, 1):
        for i in ORDER:
            for copy in stage1(route, i):
                copy.wait_recv()

    def stage2(route, j):
        to = 2 * j + (pos[route] + route) % 2
        me = pos[1 - route]
        return to == me, pltpu.make_async_remote_copy(
            part.at[route, j], parts.at[me],
            s2_send.at[route, j], s2_recv.at[me],
            {"rows": at(1 - route, to)}, MESH,
        )

    for route in (0, 1):
        names = jnp.sum(got_labels[route], axis=0)
        lane = iota((1, LANES), 1)
        target = jnp.where(names > 0.0, ((lane % (HALF * CAP)) // CAP * SHARE).astype(F32) + names - 1.0, -1.0)
        chosen = (iota((HALF * SHARE, LANES), 0).astype(F32) == target).astype(F32)
        counts = jnp.sum(chosen, axis=1, keepdims=True)
        arrived = got[route].reshape(RING * HALF * CAP, width)
        sums = jnp.dot(chosen.astype(BF16), arrived, preferred_element_type=F32)
        part[route, :, :, 0:width] = sums.reshape(HALF, SHARE, width)
        part[route, :, :, width : width + LANES] = jnp.broadcast_to(counts, (HALF * SHARE, LANES)).reshape(
            HALF, SHARE, LANES
        )
        for j in range(HALF):
            mine_too, copy = stage2(route, j)

            @pl.when(jnp.logical_not(mine_too))
            def _():
                copy.start()

            @pl.when(mine_too)
            def _():
                parts[pos[1 - route]] = part[route, j]

    for i in range(1, n_cent):
        across(0, i).start()

    mine_along = jnp.where(par == 0, z, y)
    mine_across = jnp.where(par == 0, y, z)
    for i in range(1, RING):
        src = (mine_along + i) % RING
        pltpu.make_async_remote_copy(
            part.at[0, 0], parts.at[src], s2_send.at[0, 0], s2_recv.at[src], {"rows": row}, MESH
        ).wait_recv()
    total = parts[0]
    for i in range(1, RING):
        total = total + parts[i]
    fresh = (total[:, 0:width] + cents[row].astype(F32)) / (total[:, width : width + 1] + 1.0)
    new[par, mine_across, mine_along // 2] = fresh.astype(BF16)

    def gather1(i):
        to = (mine_along + i) % RING
        who = jnp.where(par == 0, to * RING + y, z * RING + to)
        spot = new.at[par, mine_across, mine_along // 2]
        return pltpu.make_async_remote_copy(
            spot, spot, g1_send.at[i], g1_recv.at[par, mine_along // 2], {"rows": who}, MESH
        )

    for i in ORDER:
        gather1(i).start()

    def ring(route, s, d, j):
        sign = 1 - 2 * d
        spot = new.at[route, (pos[route] - sign * (s - 1)) % RING, j]
        return pltpu.make_async_remote_copy(
            spot, spot, g2_send.at[route, d, s, j], g2_recv.at[route, d, s, j],
            {"rows": at(route, (pos[route] + sign) % RING)}, MESH,
        )

    def used(s, d, j):
        return s < HALF or (j < HALF // 2) == (d == 0)

    for j in range(HALF):
        for route in (0, 1):
            src = 2 * j + (pos[route] + route) % 2

            @pl.when(src != pos[1 - route])
            def _():
                spot = new.at[route, pos[route], j]
                pltpu.make_async_remote_copy(
                    spot, spot, g1_send.at[0], g1_recv.at[route, j], {"rows": row}, MESH
                ).wait_recv()

            for d in (0, 1):
                ring(route, 1, d, j).start()
    for s in range(2, HALF + 2):
        for j in range(HALF):
            for route in (0, 1):
                for d in (0, 1):
                    if used(s - 1, d, j):
                        ring(route, s - 1, d, j).wait_recv()
                    if s <= HALF and used(s, d, j):
                        ring(route, s, d, j).start()

    def store(route, p):
        if route == 0:
            return pltpu.make_async_copy(
                new.at[0, p], updated_hbm.at[:, p % 2, p // 2, p % 2], out_sem.at[0, p]
            )
        return pltpu.make_async_copy(new.at[1, p], updated_hbm.at[p // 2, p % 2, :, 1 - p % 2], out_sem.at[1, p])

    for p in range(RING):
        for route in (0, 1):
            store(route, p).start()

    def second_tile(i, low):
        for route in (0, 1):
            block = new[route, pl.ds(i * 2, 2)].reshape(2 * HALF * SHARE, width)
            low = smallest(block, low)
        return low

    best[1] = lax.fori_loop(0, HALF, second_tile, none)
    for i in range(1, n_cent):
        across(1, i).start()
    bests[1, cent] = best[1]
    for which in (0, 1):
        for i in range(1, n_cent):
            across(which, i).wait_recv()
        low = bests[which, 0]
        for i in range(1, n_cent):
            low = jnp.minimum(low, bests[which, i])
        nearest_ref[which : which + 1, :] = (pnorm[...] + low) / width

    for route in (0, 1):
        for i in ORDER:
            for copy in stage1(route, i):
                copy.wait_send()
        for j in range(HALF):
            mine_too, copy = stage2(route, j)

            @pl.when(jnp.logical_not(mine_too))
            def _():
                copy.wait_send()

        for p in range(RING):
            store(route, p).wait()
    for i in ORDER:
        gather1(i).wait_send()
    for s in range(1, HALF + 1):
        for j in range(HALF):
            for route in (0, 1):
                for d in (0, 1):
                    if used(s, d, j):
                        ring(route, s, d, j).wait_send()
    for which in (0, 1):
        for i in range(1, n_cent):
            across(which, i).wait_send()


def solution(mesh):
    n_cent = mesh.shape["cent"]

    def per_device(points, centroids, assign):
        n_pts, width = points.shape
        dma = pltpu.SemaphoreType.DMA
        nearest, updated = pl.pallas_call(
            kernel,
            out_shape=(
                jax.ShapeDtypeStruct((2, n_pts), F32),
                jax.ShapeDtypeStruct((HALF, 2, HALF, 2, SHARE, width), BF16),
            ),
            in_specs=[
                pl.BlockSpec(memory_space=pl.ANY),
                pl.BlockSpec(memory_space=pl.ANY),
                pl.BlockSpec(memory_space=pltpu.VMEM),
            ],
            out_specs=(pl.BlockSpec(memory_space=pltpu.VMEM), pl.BlockSpec(memory_space=pl.ANY)),
            scratch_shapes=[
                pltpu.VMEM((n_pts, width), BF16),
                pltpu.VMEM((RING * RING, SHARE, width), BF16),
                pltpu.VMEM((2 * RING * HALF * CAP, n_pts), BF16),
                pltpu.VMEM((2 * RING, HALF * CAP, width), BF16),
                pltpu.VMEM((2 * RING, 1, LANES), F32),
                pltpu.VMEM((2, RING, HALF * CAP, width), BF16),
                pltpu.VMEM((2, RING, 1, LANES), F32),
                pltpu.VMEM((2, HALF, SHARE, width + LANES), F32),
                pltpu.VMEM((RING, SHARE, width + LANES), F32),
                pltpu.VMEM((2, RING, HALF, SHARE, width), BF16),
                pltpu.VMEM((2, 1, n_pts), F32),
                pltpu.VMEM((2, n_cent, 1, n_pts), F32),
                pltpu.VMEM((1, n_pts), F32),
                dma((2,)),
                dma((2, RING)),
                dma((2, RING)),
                dma((2, RING)),
                dma((2, RING)),
                dma((2, RING)),
                dma((2, HALF)),
                dma((RING,)),
                dma((RING,)),
                dma((2, HALF)),
                dma((2, 2, HALF + 1, HALF)),
                dma((2, 2, HALF + 1, HALF)),
                dma((2, n_cent)),
                dma((2, n_cent)),
            ],
            compiler_params=pltpu.CompilerParams(
                collective_id=0, has_side_effects=True, vmem_limit_bytes=60 * 1024 * 1024
            ),
        )(
            points,
            centroids.reshape(RING * RING, SHARE, width),
            assign.reshape(n_pts // LANES, LANES),
        )
        return nearest, updated.reshape(RING * RING * SHARE, width)

    return jax.shard_map(
        per_device,
        mesh=mesh,
        in_specs=(P("rows", None), P("cent", None), P("rows")),
        out_specs=(P(None, "rows"), P("cent", None)),
        check_vma=False,
    )
```

time: 95.5 us -> 67.7 us (0.71)
  Pallas kernels: 0 us -> 63.3 us
  waiting for transfers between devices: 41 us -> 0 us
  starting transfers between devices: 24.6 us -> 0 us
  blocking collectives: 13.2 us -> 0 us
  matrix products: 6.57 us -> 0 us
  other arithmetic: 5.92 us -> 0 us
    pallas_call x0 -> x1, Pallas kernels: none -> 63.3 us  [per_device(): pl.pallas_call(kernel, out_shape=(jax.ShapeDtypeStruct((2, n_pts), F32),...]
    all_to_all x2 -> x0, waiting for transfers between devices: 41 us -> none  [the longest x1 23 us: copy_for_each(): lax.all_to_all(jnp.broadcast_to(shard[None], (length, *shard.shape)), axi...]
    all_to_all x2 -> x0, starting transfers between devices: 24.6 us -> none  [the longest x1 17.1 us: in_one_piece(): lax.all_to_all(both, axis, split_axis=split_dim, concat_axis=concat_dim,...]
    all_to_all x1 -> x0, blocking collectives: 13.2 us -> none  [copy_for_each(): lax.all_to_all(jnp.broadcast_to(shard[None], (length, *shard.shape)), axi...]
    dot_general x5 -> x0, matrix products: 6.57 us -> none  [the longest x2 2.78 us: smallest(): lax.dot_general(points, cents, (((1,), (1,)), ((), ())), preferred_elemen...]
    reduce_sum x5 -> x0, other arithmetic: 2.65 us -> none  [the longest x2 1.87 us: smallest(): cnorm = jnp.sum(jnp.square(cents.astype(jnp.float32)), axis=1)]
    unnamed x5 -> x2, local copies, waits for them, and re-layouts: 0.98 us -> 3.56 us
    select_n x2 -> x0, other arithmetic: 1.4 us -> none  [the longest x1 0.7 us: per_device(): slot_index = jnp.where(inside, owners * capacity + ranking, -1)]
  transfers between devices with their start and end apart: 2 -> 0, of which waited for: 2 -> 0; matrix products, arithmetic and copies ran while one was open for 4% -> 0% of each run, Pallas kernels for 0% -> 0%
where the time goes in v1:
time: 67.7 us; the launch traced here: 67.5 us
  Pallas kernels  63.3 us (94%)
  local copies, waits for them, and re-layouts  3.56 us (5%)
    pallas_call x1, Pallas kernels, per_device(): pl.pallas_call(kernel, out_shape=(jax.ShapeDtypeStruct((2, n_pts), F32),...  63.3 us
    unnamed x2, local copies, waits for them, and re-layouts  3.56 us

profile of v1, /device:TPU:1, one launch (start us, length us, event | category | flops | bytes accessed | tf_op | source)
XLA Modules:
  0.0 67.5 jit_solution(601617504471656976)
XLA Ops:
  0.6 63.3 %shard_map.50 = (f32[2,1024]{1,0:T(2,128)}, bf16[4,2,4,2,8,1024]{5,4,3,2,1,0:T(8,128)(2,1)}) custom-call(bf16[1024,1024]{1,0:T(8,128)(2,1)} %points_hbm.1, bf16[64,8,1024]{2,1,0:T(8,128)(2,1)} %bitcast.3, s32[8,128]{1,0:T(8,128)} %bitcast.5), custom_call_target="tpu_custom_call" | custom-call | tf_op jit(solution)/shard_map/pallas_call | solution.py:327
  63.9 1.3 %copy.7 = f32[2,1024]{1,0:T(2,128)} copy(f32[2,1024]{1,0:T(2,128)} %get-tuple-element.8) | data formatting | bytes 16384
  65.2 2.3 %copy.8 = bf16[512,1024]{1,0:T(8,128)(2,1)} copy(bf16[512,1024]{1,0:T(8,128)(2,1)} %bitcast.4) | data formatting | bytes 2097152

commit v2 on v1

--- a/solution.py
+++ b/solution.py
@@ -17,6 +17,9 @@
 LANES = 128
 NT = (((1,), (1,)), ((), ()))
 ORDER = (4, 3, 5, 2, 6, 1, 7)
+ONE, TWO, THREE, FAR = range(4)
+HOPS = ((1, 0), (2, 0), (1, 2), (2, 2))
+WAVE = sorted(((s, q) for s in range(2) for q in range(HALF)), key=lambda e: 10 * e[1] + 33 * e[0])
 
 
 def iota(shape, dim):
@@ -24,9 +27,9 @@
 
 
 def kernel(
-    points_hbm, cents_hbm, assign_ref, nearest_ref, updated_hbm,
-    pts, cents, place, slots, labels, got, got_labels, part, parts, new, best, bests, pnorm,
-    local_sem, out_sem, s1_send, s1_recv, l1_send, l1_recv, s2_send, s2_recv,
+    points_hbm, cents_hbm, assign_hbm, new, bests, pnorm,
+    assigned, pts, cents, place, slots, labels, got, got_labels, part, parts, best,
+    local_sem, s1_send, s1_recv, l1_send, l1_recv, s2_send, s2_recv,
     g1_send, g1_recv, g2_send, g2_recv, c_send, c_recv,
 ):
     n_pts, width = points_hbm.shape
@@ -42,6 +45,8 @@
     def at(route, p):
         return z * RING + p if route == 0 else p * RING + y
 
+    load_assign = pltpu.make_async_copy(assign_hbm, assigned, local_sem.at[2])
+    load_assign.start()
     load_pts = pltpu.make_async_copy(points_hbm, pts, local_sem.at[0])
     load_cents = pltpu.make_async_copy(cents_hbm, cents, local_sem.at[1])
     load_pts.start()
@@ -56,7 +61,8 @@
     for i in range(1, n_cent):
         pl.semaphore_signal(barrier, inc=1, device_id={"cent": (cent + i) % n_cent}, device_id_type=MESH)
 
-    rel = assign_ref[...] - cent * (RING * RING * SHARE)
+    load_assign.wait()
+    rel = assigned[...] - cent * (RING * RING * SHARE)
     inside = (rel >= 0) & (rel < RING * RING * SHARE)
     owner = jnp.where(inside, rel // SHARE, -1)
     label = jnp.where(inside, rel % SHARE + 1, 0).astype(F32)
@@ -135,7 +141,7 @@
         got[route, pos[route]] = slots[route * RING + pos[route]]
 
     load_cents.wait()
-    chunk = 8
+    chunk = 32
 
     def smallest(block, low):
         dots = lax.dot_general(block, pts[...], NT, preferred_element_type=F32)
@@ -230,67 +236,69 @@
     for i in ORDER:
         gather1(i).start()
 
-    def ring(route, s, d, j):
+    def group(route, column, q):
+        away = pos[1 - route]
+        odd = (away + column + route) % 2
+        near, far = (0, 2, 6, 4)[q], (1, 7, 3, 5)[q]
+        return (away + near + odd * (far - near)) % RING // 2
+
+    def hop(route, kind, d, q):
         sign = 1 - 2 * d
-        spot = new.at[route, (pos[route] - sign * (s - 1)) % RING, j]
+        reach, since = HOPS[kind]
+        column = (pos[route] - sign * since) % RING
+        spot = new.at[route, column, group(route, column, q)]
         return pltpu.make_async_remote_copy(
-            spot, spot, g2_send.at[route, d, s, j], g2_recv.at[route, d, s, j],
-            {"rows": at(route, (pos[route] + sign) % RING)}, MESH,
-        )
-
-    def used(s, d, j):
-        return s < HALF or (j < HALF // 2) == (d == 0)
-
-    for j in range(HALF):
+            spot, spot, g2_send.at[route, d, kind, q], g2_recv.at[route, d, kind, q],
+            {"rows": at(route, (pos[route] + sign * reach) % RING)}, MESH,
+        )
+
+    def used(kind, d, q):
+        return kind != FAR or (q in (0, 3)) == (d == 0)
+
+    for s, q in WAVE:
         for route in (0, 1):
-            src = 2 * j + (pos[route] + route) % 2
-
-            @pl.when(src != pos[1 - route])
-            def _():
-                spot = new.at[route, pos[route], j]
-                pltpu.make_async_remote_copy(
-                    spot, spot, g1_send.at[0], g1_recv.at[route, j], {"rows": row}, MESH
-                ).wait_recv()
-
+            if s == 0:
+                j = group(route, pos[route], q)
+                fetch = pltpu.make_async_remote_copy(
+                    new.at[0, 0, 0], new.at[route, pos[route], j], g1_send.at[0], g1_recv.at[route, j],
+                    {"rows": row}, MESH,
+                )
+                if q == 0:
+                    pl.when(par != route)(fetch.wait_recv)
+                else:
+                    fetch.wait_recv()
+                for kind in (TWO, ONE):
+                    for d in (0, 1):
+                        hop(route, kind, d, q).start()
+            else:
+                for d in (0, 1):
+                    hop(route, TWO, d, q).wait_recv()
+                    for kind in (FAR, THREE):
+                        if used(kind, d, q):
+                            hop(route, kind, d, q).start()
+    for route in (0, 1):
+        for d in (0, 1):
+            for q in range(HALF):
+                hop(route, ONE, d, q).wait_recv()
+
+    def columns_of(offsets):
+        parts_of = [new[route, (pos[route] + k) % RING] for route in (0, 1) for k in offsets]
+        return jnp.concatenate(parts_of, axis=0).reshape(2 * len(offsets) * HALF * SHARE, width)
+
+    best[1] = smallest(columns_of((0, 1, 2, 6, 7)), none)
+    for q in range(HALF):
+        for route in (0, 1):
             for d in (0, 1):
-                ring(route, 1, d, j).start()
-    for s in range(2, HALF + 2):
-        for j in range(HALF):
-            for route in (0, 1):
-                for d in (0, 1):
-                    if used(s - 1, d, j):
-                        ring(route, s - 1, d, j).wait_recv()
-                    if s <= HALF and used(s, d, j):
-                        ring(route, s, d, j).start()
-
-    def store(route, p):
-        if route == 0:
-            return pltpu.make_async_copy(
-                new.at[0, p], updated_hbm.at[:, p % 2, p // 2, p % 2], out_sem.at[0, p]
-            )
-        return pltpu.make_async_copy(new.at[1, p], updated_hbm.at[p // 2, p % 2, :, 1 - p % 2], out_sem.at[1, p])
-
-    for p in range(RING):
-        for route in (0, 1):
-            store(route, p).start()
-
-    def second_tile(i, low):
-        for route in (0, 1):
-            block = new[route, pl.ds(i * 2, 2)].reshape(2 * HALF * SHARE, width)
-            low = smallest(block, low)
-        return low
-
-    best[1] = lax.fori_loop(0, HALF, second_tile, none)
+                for kind in (THREE, FAR):
+                    if used(kind, d, q):
+                        hop(route, kind, d, q).wait_recv()
+    best[1] = smallest(columns_of((3, 4, 5)), best[1])
     for i in range(1, n_cent):
         across(1, i).start()
     bests[1, cent] = best[1]
     for which in (0, 1):
         for i in range(1, n_cent):
             across(which, i).wait_recv()
-        low = bests[which, 0]
-        for i in range(1, n_cent):
-            low = jnp.minimum(low, bests[which, i])
-        nearest_ref[which : which + 1, :] = (pnorm[...] + low) / width
 
     for route in (0, 1):
         for i in ORDER:
@@ -303,40 +311,56 @@
             def _():
                 copy.wait_send()
 
-        for p in range(RING):
-            store(route, p).wait()
     for i in ORDER:
         gather1(i).wait_send()
-    for s in range(1, HALF + 1):
-        for j in range(HALF):
-            for route in (0, 1):
-                for d in (0, 1):
-                    if used(s, d, j):
-                        ring(route, s, d, j).wait_send()
+    for q in range(HALF):
+        for route in (0, 1):
+            for d in (0, 1):
+                for kind in range(len(HOPS)):
+                    if used(kind, d, q):
+                        hop(route, kind, d, q).wait_send()
     for which in (0, 1):
         for i in range(1, n_cent):
             across(which, i).wait_send()
 
 
+def finish(new, bests, pnorm, nearest, updated_hbm, out_sem):
+    copies = []
+    for p in range(RING):
+        copies.append(pltpu.make_async_copy(new.at[0, p], updated_hbm.at[:, p % 2, p // 2, p % 2], out_sem.at[0, p]))
+        copies.append(
+            pltpu.make_async_copy(new.at[1, p], updated_hbm.at[p // 2, p % 2, :, 1 - p % 2], out_sem.at[1, p])
+        )
+    for copy in copies:
+        copy.start()
+    for which in (0, 1):
+        low = bests[which, 0]
+        for i in range(1, bests.shape[1]):
+            low = jnp.minimum(low, bests[which, i])
+        nearest[which : which + 1, :] = (pnorm[...] + low) / new.shape[-1]
+    for copy in copies:
+        copy.wait()
+
+
 def solution(mesh):
     n_cent = mesh.shape["cent"]
 
     def per_device(points, centroids, assign):
         n_pts, width = points.shape
         dma = pltpu.SemaphoreType.DMA
-        nearest, updated = pl.pallas_call(
+        any_space = pl.BlockSpec(memory_space=pltpu.HBM)
+        vmem = pl.BlockSpec(memory_space=pltpu.VMEM)
+        new, bests, pnorm = pl.pallas_call(
             kernel,
             out_shape=(
-                jax.ShapeDtypeStruct((2, n_pts), F32),
-                jax.ShapeDtypeStruct((HALF, 2, HALF, 2, SHARE, width), BF16),
+                pltpu.VMEM((2, RING, HALF, SHARE, width), BF16),
+                pltpu.VMEM((2, n_cent, 1, n_pts), F32),
+                pltpu.VMEM((1, n_pts), F32),
             ),
-            in_specs=[
-                pl.BlockSpec(memory_space=pl.ANY),
-                pl.BlockSpec(memory_space=pl.ANY),
-                pl.BlockSpec(memory_space=pltpu.VMEM),
-            ],
-            out_specs=(pl.BlockSpec(memory_space=pltpu.VMEM), pl.BlockSpec(memory_space=pl.ANY)),
+            in_specs=[any_space] * 3,
+            out_specs=(vmem,) * 3,
             scratch_shapes=[
+                pltpu.VMEM((n_pts // LANES, LANES), jnp.int32),
                 pltpu.VMEM((n_pts, width), BF16),
                 pltpu.VMEM((RING * RING, SHARE, width), BF16),
                 pltpu.VMEM((2 * RING * HALF * CAP, n_pts), BF16),
@@ -346,12 +370,8 @@
                 pltpu.VMEM((2, RING, 1, LANES), F32),
                 pltpu.VMEM((2, HALF, SHARE, width + LANES), F32),
                 pltpu.VMEM((RING, SHARE, width + LANES), F32),
-                pltpu.VMEM((2, RING, HALF, SHARE, width), BF16),
                 pltpu.VMEM((2, 1, n_pts), F32),
-                pltpu.VMEM((2, n_cent, 1, n_pts), F32),
-                pltpu.VMEM((1, n_pts), F32),
-                dma((2,)),
-                dma((2, RING)),
+                dma((3,)),
                 dma((2, RING)),
                 dma((2, RING)),
                 dma((2, RING)),
@@ -360,19 +380,35 @@
                 dma((RING,)),
                 dma((RING,)),
                 dma((2, HALF)),
-                dma((2, 2, HALF + 1, HALF)),
-                dma((2, 2, HALF + 1, HALF)),
+                dma((2, 2, len(HOPS), HALF)),
+                dma((2, 2, len(HOPS), HALF)),
                 dma((2, n_cent)),
                 dma((2, n_cent)),
             ],
             compiler_params=pltpu.CompilerParams(
-                collective_id=0, has_side_effects=True, vmem_limit_bytes=60 * 1024 * 1024
+                collective_id=0, has_side_effects=True, vmem_limit_bytes=40 * 1024 * 1024
             ),
         )(
-            points,
-            centroids.reshape(RING * RING, SHARE, width),
-            assign.reshape(n_pts // LANES, LANES),
-        )
+            *(
+                pltpu.with_memory_space_constraint(a, pltpu.HBM)
+                for a in (
+                    points,
+                    centroids.reshape(RING * RING, SHARE, width),
+                    assign.reshape(n_pts // LANES, LANES),
+                )
+            )
+        )
+        nearest, updated = pl.pallas_call(
+            finish,
+            out_shape=(
+                jax.ShapeDtypeStruct((2, n_pts), F32),
+                jax.ShapeDtypeStruct((HALF, 2, HALF, 2, SHARE, width), BF16),
+            ),
+            in_specs=[vmem] * 3,
+            out_specs=(vmem, any_space),
+            scratch_shapes=[dma((2, RING))],
+            compiler_params=pltpu.CompilerParams(vmem_limit_bytes=16 * 1024 * 1024),
+        )(new, bests, pnorm)
         return nearest, updated.reshape(RING * RING * SHARE, width)
 
     return jax.shard_map(

time: 67.7 us -> 55.4 us (0.82)
  Pallas kernels: 63.3 us -> 54.6 us
  local copies, waits for them, and re-layouts: 3.56 us -> 0 us
    pallas_call x1 -> x2, Pallas kernels: 63.3 us -> 54.6 us  [the longest x1 53 us: per_device(): pl.pallas_call(kernel, out_shape=(pltpu.VMEM((2, RING, HALF, SHARE, width...]
    unnamed x2 -> x0, local copies, waits for them, and re-layouts: 3.56 us -> none
where the time goes in v2:
time: 55.4 us; the launch traced here: 55.3 us
  Pallas kernels  54.6 us (99%)
  between operations  0.64 us (1%)
    pallas_call x1, Pallas kernels, per_device(): pl.pallas_call(kernel, out_shape=(pltpu.VMEM((2, RING, HALF, SHARE, width...  53 us
    pallas_call x1, Pallas kernels, per_device(): pl.pallas_call(finish, out_shape=(jax.ShapeDtypeStruct((2, n_pts), F32),...  1.69 us

profile of v2, /device:TPU:1, one launch (start us, length us, event | category | flops | bytes accessed | tf_op | source)
XLA Modules:
  0.0 55.3 jit_solution(1862378349059626849)
XLA Ops:
  0.6 53.0 %shard_map.50 = (bf16[2,8,4,8,1024]{4,3,2,1,0:T(8,128)(2,1)S(1)}, f32[2,8,1,1024]{3,2,1,0:T(1,128)S(1)}, f32[1,1024]{1,0:T(1,128)S(1)}) custom-call(bf16[1024,1024]{1,0:T(8,128)(2,1)} %points_hbm.1, bf16[64,8,1024]{2,1,0:T(8,128)(2,1)} %bitcast.3, s32[8,128]{1,0:T(8,128)} %bitcast.4), custom_call_target="tpu_custom_call" | custom-call | tf_op jit(solution)/shard_map/pallas_call | solution.py:353
  53.6 1.7 %shard_map.51 = (f32[2,1024]{1,0:T(2,128)}, bf16[4,2,4,2,8,1024]{5,4,3,2,1,0:T(8,128)(2,1)}) custom-call(bf16[2,8,4,8,1024]{4,3,2,1,0:T(8,128)(2,1)S(1)} %get-tuple-element.7.new, f32[2,8,1,1024]{3,2,1,0:T(1,128)S(1)} %get-tuple-element.8.bests, f32[1,1024]{1,0:T(1,128)S(1)} %get-tuple-element.9.pnorm), custom_call_target="tpu_custom_call" | custom-call | tf_op jit(solution)/shard_map/pallas_call | solution.py:401

commit v3 on v2

v3 whole, which is shorter than its diff:
```python
import functools

import jax
import jax.numpy as jnp
from jax import lax
from jax.experimental import pallas as pl
from jax.experimental.pallas import tpu as pltpu
from jax.sharding import PartitionSpec as P

MESH = pl.DeviceIdType.MESH
F32 = jnp.float32
BF16 = jnp.bfloat16
RING = 8
HALF = RING // 2
SHARE = 8
CAP = 4
CUTS = 2
LANES = 128
NT = (((1,), (1,)), ((), ()))
ORDER = (4, 3, 5, 2, 6, 1, 7)
ONE, THREE, FAR, TWO = range(4)
HOPS = ((1, 0), (1, 2), (2, 2), (2, 0))
LABELS, STAGE1, STAGE2, COUNTS, GATHER1, GATHER2, ACROSS = range(7)
WAVE = sorted(
    ((s, f, q) for s in range(2) for f in range(CUTS) for q in range(HALF)),
    key=lambda e: 33 * e[0] + 20 * e[1] + 10 * e[2],
)


def iota(shape, dim):
    return lax.broadcasted_iota(jnp.int32, shape, dim)


def kernel(
    points_hbm, cents_hbm, assign_hbm, new, bests, pnorm,
    assigned, pts, cents, place, slots, labels, got, got_labels, part, parts, part_counts, counts_in, best,
    local_sem, sent, l1_recv, s1_recv, s2_recv, g1_recv, two_recv, rest_recv, c_recv,
):
    n_pts, width = points_hbm.shape
    blocks = n_pts // LANES
    cut = width // CUTS
    row = lax.axis_index("rows")
    cent = lax.axis_index("cent")
    z = row // RING
    y = row % RING
    par = (z + y) % 2
    pos = (y, z)
    n_cent = bests.shape[1]

    def awaited(ref, sem):
        return pltpu.make_async_remote_copy(ref, ref, sem, sem, {"rows": row}, MESH)

    def at(route, p):
        return z * RING + p if route == 0 else p * RING + y

    load_assign = pltpu.make_async_copy(assign_hbm, assigned, local_sem.at[2])
    load_assign.start()
    load_pts = pltpu.make_async_copy(points_hbm, pts, local_sem.at[0])
    load_cents = pltpu.make_async_copy(cents_hbm, cents, local_sem.at[1])
    load_pts.start()
    load_cents.start()

    barrier = pltpu.get_barrier_semaphore()
    for route in (0, 1):
        for i in ORDER:
            pl.semaphore_signal(
                barrier, inc=1, device_id={"rows": at(route, (pos[route] + i) % RING)}, device_id_type=MESH
            )
    for i in range(1, n_cent):
        pl.semaphore_signal(barrier, inc=1, device_id={"cent": (cent + i) % n_cent}, device_id_type=MESH)

    load_assign.wait()
    rel = assigned[...] - cent * (RING * RING * SHARE)
    inside = (rel >= 0) & (rel < RING * RING * SHARE)
    owner = jnp.where(inside, rel // SHARE, -1)
    label = jnp.where(inside, rel % SHARE + 1, 0).astype(F32)
    oz = owner // RING
    oy = owner % RING
    kind = (oz + oy) % 2
    prim = jnp.where(kind == 0, oy, oz)
    sec = jnp.where(kind == 0, oz, oy) // 2
    me_lane = jnp.where(kind == 0, y, z) * (HALF * CAP)

    groups = iota((RING * RING, LANES), 0)
    hots = [(groups == owner[b : b + 1, :]).astype(F32) for b in range(blocks)]
    upper = (iota((LANES, LANES), 0) < iota((LANES, LANES), 1)).astype(BF16)
    within = jnp.dot(
        jnp.concatenate(hots, axis=0).astype(BF16), upper, preferred_element_type=F32
    )
    carry = jnp.zeros((RING * RING, 1), F32)
    marks, spots = [], []
    for b in range(blocks):
        before = within[b * RING * RING : (b + 1) * RING * RING] + carry
        rank = jnp.sum(hots[b] * before, axis=0, keepdims=True).astype(jnp.int32)
        carry = carry + jnp.sum(hots[b], axis=1, keepdims=True)
        ins, knd, prm = inside[b : b + 1, :], kind[b : b + 1, :], prim[b : b + 1, :]
        spot = sec[b : b + 1, :] * CAP + rank
        slot = jnp.where(ins, (knd * RING + prm) * (HALF * CAP) + spot, -1)
        columns = slice(b * LANES, (b + 1) * LANES)
        place[:, columns] = (iota((place.shape[0], LANES), 0) == slot).astype(F32).astype(BF16)
        marks.append(
            jnp.where(
                iota((2 * RING, LANES), 0) == jnp.where(ins, knd * RING + prm, -1), label[b : b + 1, :], 0.0
            )
        )
        spots.append((iota((LANES, LANES), 0) == me_lane[b : b + 1, :] + spot).astype(F32))
    mine = lax.dot_general(
        jnp.concatenate(marks, axis=1).astype(BF16),
        jnp.concatenate(spots, axis=1).astype(BF16),
        NT,
        preferred_element_type=F32,
    )
    for d in range(2 * RING):
        labels[d] = mine[d : d + 1, :]

    load_pts.wait()
    tile = 256

    def place_tile(i, _):
        columns = pl.ds(pl.multiple_of(i * tile, tile), tile)
        rows = jnp.dot(place[...], pts[:, columns], preferred_element_type=F32).astype(BF16)
        steps = cut // tile
        slots[i // steps, :, :, pl.ds(pl.multiple_of(i % steps * tile, tile), tile)] = rows.reshape(
            2 * RING, HALF * CAP, tile
        )
        return 0

    def label_copy(route, i):
        to = (pos[route] + i) % RING
        return pltpu.make_async_remote_copy(
            labels.at[route * RING + to], got_labels.at[route, pos[route]],
            sent.at[LABELS], l1_recv.at[0], {"rows": at(route, to)}, MESH,
        )

    def stage1(f, route, i):
        to = (pos[route] + i) % RING
        return pltpu.make_async_remote_copy(
            slots.at[f, route * RING + to], got.at[f, route, pos[route]],
            sent.at[STAGE1], s1_recv.at[f, route], {"rows": at(route, to)}, MESH,
        )

    for f in range(CUTS):
        lax.fori_loop(f * (cut // tile), (f + 1) * (cut // tile), place_tile, 0)
        if f == 0:
            pl.semaphore_wait(barrier, 2 * (RING - 1) + n_cent - 1)
            for i in ORDER:
                for route in (0, 1):
                    label_copy(route, i).start()
        for i in ORDER:
            for route in (0, 1):
                stage1(f, route, i).start()
    for route in (0, 1):
        got_labels[route, pos[route]] = labels[route * RING + pos[route]]
        for f in range(CUTS):
            got[f, route, pos[route]] = slots[f, route * RING + pos[route]]

    load_cents.wait()
    chunk = 32

    def smallest(blocks_of, low):
        dots, norm = 0.0, 0.0
        for f, block in enumerate(blocks_of):
            step = width // len(blocks_of)
            dots += lax.dot_general(
                block, pts[:, f * step : (f + 1) * step], NT, preferred_element_type=F32
            )
            wide = block.astype(F32)
            norm += jnp.sum(wide * wide, axis=1, keepdims=True)
        return jnp.minimum(low, jnp.min(norm - 2.0 * dots, axis=0, keepdims=True))

    def first_tile(i, low):
        block = cents[pl.ds(i * chunk, chunk)].reshape(chunk * SHARE, width)
        return smallest([block], low)

    none = jnp.full((1, n_pts), jnp.inf, F32)
    best[0] = lax.fori_loop(0, RING * RING // chunk, first_tile, none)
    bests[0, cent] = best[0]

    def norm_tile(i, _):
        rows = pl.ds(pl.multiple_of(i * LANES, LANES), LANES)
        wide = pts[rows, :].astype(F32)
        total = jnp.sum(wide * wide, axis=1, keepdims=True)
        pnorm[:, rows] = jnp.transpose(jnp.broadcast_to(total, (LANES, LANES)))[0:1, :]
        return 0

    lax.fori_loop(0, blocks, norm_tile, 0)

    def stage2(f, route, j):
        to = 2 * j + (pos[route] + route) % 2
        me = pos[1 - route]
        return to == me, (
            pltpu.make_async_remote_copy(
                part.at[f, route, j], parts.at[f, me], sent.at[STAGE2], s2_recv.at[f],
                {"rows": at(1 - route, to)}, MESH,
            ),
            pltpu.make_async_remote_copy(
                part_counts.at[route, j], counts_in.at[me], sent.at[COUNTS], s2_recv.at[CUTS],
                {"rows": at(1 - route, to)}, MESH,
            ),
        )

    hot = [None, None]
    for f in range(CUTS):
        for route in (0, 1):
            if f == 0 and route == 0:
                awaited(got_labels.at[:, 0 : RING - 1], l1_recv.at[0]).wait_recv()
            awaited(got.at[f, route, 0 : RING - 1], s1_recv.at[f, route]).wait_recv()
            if f == 0:
                names = jnp.sum(got_labels[route], axis=0)
                lane = iota((1, LANES), 1)
                target = jnp.where(
                    names > 0.0, ((lane % (HALF * CAP)) // CAP * SHARE).astype(F32) + names - 1.0, -1.0
                )
                chosen = (iota((HALF * SHARE, LANES), 0).astype(F32) == target).astype(F32)
                hot[route] = chosen.astype(BF16)
                counts = jnp.sum(chosen, axis=1, keepdims=True)
                part_counts[route] = jnp.broadcast_to(counts, (HALF * SHARE, LANES)).reshape(HALF, SHARE, LANES)
            sums = jnp.dot(
                hot[route], got[f, route].reshape(RING * HALF * CAP, cut), preferred_element_type=F32
            )
            part[f, route] = sums.reshape(HALF, SHARE, cut)
            for j in range(HALF):
                mine_too, copies = stage2(f, route, j)

                @pl.when(jnp.logical_not(mine_too))
                def _():
                    if f == 0:
                        copies[1].start()
                    copies[0].start()

                @pl.when(mine_too)
                def _():
                    if f == 0:
                        counts_in[pos[1 - route]] = part_counts[route, j]
                    parts[f, pos[1 - route]] = part[f, route, j]

    def across(which, i):
        return pltpu.make_async_remote_copy(
            best.at[which], bests.at[which, cent], sent.at[ACROSS], c_recv.at[which],
            {"cent": (cent + i) % n_cent}, MESH,
        )

    for i in range(1, n_cent):
        across(0, i).start()

    mine_along = jnp.where(par == 0, z, y)
    mine_across = jnp.where(par == 0, y, z)

    def gather1(f, i):
        to = (mine_along + i) % RING
        who = jnp.where(par == 0, to * RING + y, z * RING + to)
        spot = new.at[f, par, mine_across, mine_along // 2]
        return pltpu.make_async_remote_copy(
            spot, spot, sent.at[GATHER1], g1_recv.at[f, par, mine_along // 2], {"rows": who}, MESH
        )

    for f in range(CUTS):
        if f == 0:
            awaited(counts_in.at[0 : RING - 1], s2_recv.at[CUTS]).wait_recv()
        awaited(parts.at[f, 0 : RING - 1], s2_recv.at[f]).wait_recv()
        total = parts[f, 0]
        for i in range(1, RING):
            total = total + parts[f, i]
        if f == 0:
            count = counts_in[0]
            for i in range(1, RING):
                count = count + counts_in[i]
            count = count[:, 0:1] + 1.0
        own = cents[row][:, f * cut : (f + 1) * cut].astype(F32)
        new[f, par, mine_across, mine_along // 2] = ((total + own) / count).astype(BF16)
        for i in ORDER:
            gather1(f, i).start()

    def group(route, column, q):
        away = pos[1 - route]
        odd = (away + column + route) % 2
        near, far = (0, 2, 6, 4)[q], (1, 7, 3, 5)[q]
        return (away + near + odd * (far - near)) % RING // 2

    def hop(f, route, kind, d, q):
        sign = 1 - 2 * d
        reach, since = HOPS[kind]
        column = (pos[route] - sign * since) % RING
        spot = new.at[f, route, column, group(route, column, q)]
        return pltpu.make_async_remote_copy(
            spot, spot, sent.at[GATHER2], two_recv.at[f, route, q] if kind == TWO else rest_recv.at[min(kind, 1)],
            {"rows": at(route, (pos[route] + sign * reach) % RING)}, MESH,
        )

    def used(kind, d, q):
        return kind != FAR or (q in (0, 3)) == (d == 0)

    for s, f, q in WAVE:
        for route in (0, 1):
            if s == 0:
                j = group(route, pos[route], q)
                fetch = awaited(new.at[f, route, pos[route], j], g1_recv.at[f, route, j])
                if q == 0:
                    pl.when(par != route)(fetch.wait_recv)
                else:
                    fetch.wait_recv()
                for kind in (TWO, ONE):
                    for d in (0, 1):
                        hop(f, route, kind, d, q).start()
            else:
                awaited(new.at[f, route, 0, 0:2], two_recv.at[f, route, q]).wait_recv()
                for d in (0, 1):
                    for kind in (FAR, THREE):
                        if used(kind, d, q):
                            hop(f, route, kind, d, q).start()
    awaited(new.at[:, :, 0:2], rest_recv.at[0]).wait_recv()

    def columns_of(offsets):
        blocks_of = []
        for f in range(CUTS):
            picked = [new[f, route, (pos[route] + k) % RING] for route in (0, 1) for k in offsets]
            blocks_of.append(jnp.concatenate(picked, axis=0).reshape(2 * len(offsets) * HALF * SHARE, cut))
        return blocks_of

    best[1] = smallest(columns_of((0, 1, 2, 6, 7)), none)
    awaited(new.at[:, :, 0:3], rest_recv.at[1]).wait_recv()
    best[1] = smallest(columns_of((3, 4, 5)), best[1])
    for i in range(1, n_cent):
        across(1, i).start()
    bests[1, cent] = best[1]
    for which in (0, 1):
        awaited(bests.at[which, 0 : n_cent - 1], c_recv.at[which]).wait_recv()

    awaited(got_labels.at[:, 0 : RING - 1], sent.at[LABELS]).wait_send()
    awaited(got.at[:, :, 0 : RING - 1], sent.at[STAGE1]).wait_send()
    awaited(parts.at[:, 0 : RING - 1], sent.at[STAGE2]).wait_send()
    awaited(counts_in.at[0 : RING - 1], sent.at[COUNTS]).wait_send()
    awaited(new.at[:, 0, 0 : RING - 1, 0], sent.at[GATHER1]).wait_send()
    awaited(new.at[:, :, 0 : RING - 1], sent.at[GATHER2]).wait_send()
    awaited(bests.at[:, 0 : n_cent - 1], sent.at[ACROSS]).wait_send()


def finish(new, bests, pnorm, nearest, updated_hbm, out_sem):
    cut = new.shape[-1]
    for f in range(CUTS):
        columns = pl.ds(f * cut, cut)
        for p in range(RING):
            spots = (
                updated_hbm.at[:, p % 2, p // 2, p % 2, :, columns],
                updated_hbm.at[p // 2, p % 2, :, 1 - p % 2, :, columns],
            )
            for route in (0, 1):
                pltpu.make_async_copy(new.at[f, route, p], spots[route], out_sem).start()
    for which in (0, 1):
        low = bests[which, 0]
        for i in range(1, bests.shape[1]):
            low = jnp.minimum(low, bests[which, i])
        nearest[which : which + 1, :] = (pnorm[...] + low) / (CUTS * cut)
    pltpu.make_async_copy(new, new, out_sem).wait()


def solution(mesh):
    n_cent = mesh.shape["cent"]

    def per_device(points, centroids, assign):
        n_pts, width = points.shape
        cut = width // CUTS
        dma = pltpu.SemaphoreType.DMA
        any_space = pl.BlockSpec(memory_space=pltpu.HBM)
        vmem = pl.BlockSpec(memory_space=pltpu.VMEM)
        new, bests, pnorm = pl.pallas_call(
            kernel,
            out_shape=(
                pltpu.VMEM((CUTS, 2, RING, HALF, SHARE, cut), BF16),
                pltpu.VMEM((2, n_cent, 1, n_pts), F32),
                pltpu.VMEM((1, n_pts), F32),
            ),
            in_specs=[any_space] * 3,
            out_specs=(vmem,) * 3,
            scratch_shapes=[
                pltpu.VMEM((n_pts // LANES, LANES), jnp.int32),
                pltpu.VMEM((n_pts, width), BF16),
                pltpu.VMEM((RING * RING, SHARE, width), BF16),
                pltpu.VMEM((2 * RING * HALF * CAP, n_pts), BF16),
                pltpu.VMEM((CUTS, 2 * RING, HALF * CAP, cut), BF16),
                pltpu.VMEM((2 * RING, 1, LANES), F32),
                pltpu.VMEM((CUTS, 2, RING, HALF * CAP, cut), BF16),
                pltpu.VMEM((2, RING, 1, LANES), F32),
                pltpu.VMEM((CUTS, 2, HALF, SHARE, cut), F32),
                pltpu.VMEM((CUTS, RING, SHARE, cut), F32),
                pltpu.VMEM((2, HALF, SHARE, LANES), F32),
                pltpu.VMEM((RING, SHARE, LANES), F32),
                pltpu.VMEM((2, 1, n_pts), F32),
                dma((3,)),
                dma((ACROSS + 1,)),
                dma((1,)),
                dma((CUTS, 2)),
                dma((CUTS + 1,)),
                dma((CUTS, 2, HALF)),
                dma((CUTS, 2, HALF)),
                dma((2,)),
                dma((2,)),
            ],
            compiler_params=pltpu.CompilerParams(
                collective_id=0, has_side_effects=True, vmem_limit_bytes=40 * 1024 * 1024
            ),
        )(
            *(
                pltpu.with_memory_space_constraint(a, pltpu.HBM)
                for a in (
                    points,
                    centroids.reshape(RING * RING, SHARE, width),
                    assign.reshape(n_pts // LANES, LANES),
                )
            )
        )
        nearest, updated = pl.pallas_call(
            finish,
            out_shape=(
                jax.ShapeDtypeStruct((2, n_pts), F32),
                jax.ShapeDtypeStruct((HALF, 2, HALF, 2, SHARE, width), BF16),
            ),
            in_specs=[vmem] * 3,
            out_specs=(vmem, any_space),
            scratch_shapes=[dma],
            compiler_params=pltpu.CompilerParams(vmem_limit_bytes=16 * 1024 * 1024),
        )(new, bests, pnorm)
        return nearest, updated.reshape(RING * RING * SHARE, width)

    return jax.shard_map(
        per_device,
        mesh=mesh,
        in_specs=(P("rows", None), P("cent", None), P("rows")),
        out_specs=(P(None, "rows"), P("cent", None)),
        check_vma=False,
    )
```

time: 55.4 us -> 51.2 us (0.924)
  Pallas kernels: 54.6 us -> 50.4 us
    pallas_call x1, Pallas kernels: 53 us -> 48.9 us  [per_device(): pl.pallas_call(kernel, out_shape=(pltpu.VMEM((CUTS, 2, RING, HALF, SHARE,...]
where the time goes in v3:
time: 51.2 us; the launch traced here: 51.1 us
  Pallas kernels  50.4 us (98%)
  between operations  0.64 us (1%)
    pallas_call x1, Pallas kernels, per_device(): pl.pallas_call(kernel, out_shape=(pltpu.VMEM((CUTS, 2, RING, HALF, SHARE,...  48.9 us
    pallas_call x1, Pallas kernels, per_device(): pl.pallas_call(finish, out_shape=(jax.ShapeDtypeStruct((2, n_pts), F32),...  1.55 us

profile of v3, /device:TPU:1, one launch (start us, length us, event | category | flops | bytes accessed | tf_op | source)
XLA Modules:
  0.0 51.1 jit_solution(15413427471612802813)
XLA Ops:
  0.6 48.9 %shard_map.50 = (bf16[2,2,8,4,8,512]{5,4,3,2,1,0:T(8,128)(2,1)S(1)}, f32[2,8,1,1024]{3,2,1,0:T(1,128)S(1)}, f32[1,1024]{1,0:T(1,128)S(1)}) custom-call(bf16[1024,1024]{1,0:T(8,128)(2,1)} %points_hbm.1, bf16[64,8,1024]{2,1,0:T(8,128)(2,1)} %bitcast.3, s32[8,128]{1,0:T(8,128)} %bitcast.4), custom_call_target="tpu_custom_call" | custom-call | tf_op jit(solution)/shard_map/pallas_call | solution.py:366
  49.5 1.5 %shard_map.51 = (f32[2,1024]{1,0:T(2,128)}, bf16[4,2,4,2,8,1024]{5,4,3,2,1,0:T(8,128)(2,1)}) custom-call(bf16[2,2,8,4,8,512]{5,4,3,2,1,0:T(8,128)(2,1)S(1)} %get-tuple-element.7.new, f32[2,8,1,1024]{3,2,1,0:T(1,128)S(1)} %get-tuple-element.8.bests, f32[1,1024]{1,0:T(1,128)S(1)} %get-tuple-element.9.pnorm), custom_call_target="tpu_custom_call" | custom-call | tf_op jit(solution)/shard_map/pallas_call | solution.py:412
